TPU v7x, 256 devices: a whole 4x4x8 slice. The times are simulated.
256 devices in a mesh: terms: 256 (over z, y, x, core).
Axes of the slice: x: 4, y: 4, z: 8, core: 2. Of those that a mesh axis runs over, the one named last changes fastest.
Arguments:
- psi_init: float32 [256, 4, 4, 256], replicated
- left_env: bfloat16 [1536, 256, 256], P('terms')
- op_pair: bfloat16 [1536, 16, 16], P('terms')
- right_env: bfloat16 [1536, 256, 256], P('terms')
Outputs:
- output 1: float32 [7, 256, 4, 4, 256], P(None, 'terms')
- output 2: float32 [6], replicated
- output 3: float32 [6], replicated
All inputs are finite; a program needn't handle non-finite values.
Results may differ from a plain program's by a relative error of at most 0.0176077.
Values are sent between devices in bfloat16 or wider.
A program may use at most 768 MiB of HBM per device.

v0:
```python
import jax
import jax.numpy as jnp
from jax import lax
from jax.sharding import PartitionSpec as P

KRYLOV_STEPS = 6


def solution(mesh):
    group_size = mesh.shape['terms']

    def local_run(psi_init, left_env, op_pair, right_env):
        bond_dim = psi_init.shape[0]
        phys_dim = psi_init.shape[1]
        pair_dim = phys_dim * phys_dim
        elem_count = bond_dim * pair_dim * bond_dim
        slab_rows = bond_dim // group_size
        row_start = lax.axis_index('terms') * slab_rows
        psi_full = psi_init.reshape(bond_dim, pair_dim, bond_dim)
        full_norm = jnp.sqrt(jnp.sum(psi_full * psi_full) / elem_count)
        vector = lax.dynamic_slice_in_dim(psi_full, row_start, slab_rows, 0) / full_norm
        vectors = [vector]
        alphas = []
        betas = []
        prev_vector = vector
        for step_idx in range(KRYLOV_STEPS):
            whole_vector = lax.all_gather(vector.astype(jnp.bfloat16), 'terms', axis=0, tiled=True)
            y_part = jnp.einsum('apc,kbc->kapb', whole_vector, right_env, preferred_element_type=jnp.float32).astype(jnp.bfloat16)
            z_part = jnp.einsum('kqp,kapb->kaqb', op_pair, y_part, preferred_element_type=jnp.float32).astype(jnp.bfloat16)
            partial_sigma = jnp.einsum('kax,kxqb->aqb', left_env, z_part, preferred_element_type=jnp.float32)
            sigma_slab = lax.psum_scatter(partial_sigma, 'terms', scatter_dimension=0, tiled=True)
            alpha_val = lax.psum(jnp.sum(sigma_slab * vector), 'terms') / elem_count
            residual = sigma_slab - alpha_val * vector
            if step_idx > 0:
                residual = residual - betas[-1] * prev_vector
            beta_val = jnp.sqrt(lax.psum(jnp.sum(residual * residual), 'terms') / elem_count)
            prev_vector = vector
            vector = residual / beta_val
            vectors.append(vector)
            alphas.append(alpha_val)
            betas.append(beta_val)
        krylov_vectors = jnp.stack(vectors).reshape(KRYLOV_STEPS + 1, slab_rows, phys_dim, phys_dim, bond_dim)
        return krylov_vectors, jnp.stack(alphas), jnp.stack(betas)

    return jax.shard_map(local_run, mesh=mesh, in_specs=(P(), P('terms'), P('terms'), P('terms')), out_specs=(P(None, 'terms'), P(), P()), check_vma=False)
```

profile of v0, /device:TPU:1, one launch (start us, length us, event | category | flops | bytes accessed | tf_op | source)
XLA Modules:
  0.0 9579.6 jit_solution(16687991689246753130)
XLA Ops:
  19.6 108.3 %all-gather.7.cloned.1.call-done = bf16[256,16,256]{2,1,0:T(8,128)(2,1)} async-done(((bf16[1,16,256]{2,1,0:T(8,128)(2,1)}), bf16[256,16,256]{2,1,0:T(8,128)(2,1)}) %all-gather.7.cloned.1.call-update) | async-done | bytes 2097168 | tf_op jit(solution)/shard_map/all_gather | solution.py:27
  153.0 19.8 fusion.36
  178.4 1283.7 %reduce-scatter.7.cloned.1.call-done = f32[1,16,256]{2,1,0:T(8,128)} async-done(((f32[256,16,256]{2,1,0:T(8,128)}), f32[1,16,256]{2,1,0:T(8,128)}) %reduce-scatter.7.cloned.1.call-update) | async-done | bytes 16400 | tf_op jit(solution)/shard_map/reduce_scatter | solution.py:31
  1463.4 78.2 psum.84
  1543.6 74.2 psum.85
  1619.9 100.0 %all-gather.9.cloned.1.call-done = bf16[256,16,256]{2,1,0:T(8,128)(2,1)} async-done(((bf16[1,16,256]{2,1,0:T(8,128)(2,1)}), bf16[256,16,256]{2,1,0:T(8,128)(2,1)}) %all-gather.9.cloned.1.call-update) | async-done | bytes 2097168 | tf_op jit(solution)/shard_map/all_gather | solution.py:27
  1729.4 15.7 convert_bitcast_fusion.8
  1745.1 19.7 fusion.39
  1770.4 1280.9 %reduce-scatter.9.cloned.1.call-done = f32[1,16,256]{2,1,0:T(8,128)} async-done(((f32[256,16,256]{2,1,0:T(8,128)}), f32[1,16,256]{2,1,0:T(8,128)}) %reduce-scatter.9.cloned.1.call-update) | async-done | bytes 16400 | tf_op jit(solution)/shard_map/reduce_scatter | solution.py:31
  3052.6 79.7 psum.86
  3134.3 72.8 psum.87
  3208.5 100.6 %all-gather.11.cloned.1.call-done = bf16[256,16,256]{2,1,0:T(8,128)(2,1)} async-done(((bf16[1,16,256]{2,1,0:T(8,128)(2,1)}), bf16[256,16,256]{2,1,0:T(8,128)(2,1)}) %all-gather.11.cloned.1.call-update) | async-done | bytes 2097168 | tf_op jit(solution)/shard_map/all_gather | solution.py:27
  3334.1 20.0 fusion.42
  3359.6 1283.7 %reduce-scatter.11.cloned.1.call-done = f32[1,16,256]{2,1,0:T(8,128)} async-done(((f32[256,16,256]{2,1,0:T(8,128)}), f32[1,16,256]{2,1,0:T(8,128)}) %reduce-scatter.11.cloned.1.call-update) | async-done | bytes 16400 | tf_op jit(solution)/shard_map/reduce_scatter | solution.py:31
  4644.7 78.1 psum.88
  4724.7 74.3 psum.89
  4800.4 100.0 %all-gather.13.cloned.1.call-done = bf16[256,16,256]{2,1,0:T(8,128)(2,1)} async-done(((bf16[1,16,256]{2,1,0:T(8,128)(2,1)}), bf16[256,16,256]{2,1,0:T(8,128)(2,1)}) %all-gather.13.cloned.1.call-update) | async-done | bytes 2097168 | tf_op jit(solution)/shard_map/all_gather | solution.py:27
  4925.4 19.8 fusion.45
  4950.7 1280.9 %reduce-scatter.13.cloned.1.call-done = f32[1,16,256]{2,1,0:T(8,128)} async-done(((f32[256,16,256]{2,1,0:T(8,128)}), f32[1,16,256]{2,1,0:T(8,128)}) %reduce-scatter.13.cloned.1.call-update) | async-done | bytes 16400 | tf_op jit(solution)/shard_map/reduce_scatter | solution.py:31
  6232.9 81.0 psum.90
  6315.9 72.7 psum.91
  6390.0 100.7 %all-gather.15.cloned.1.call-done = bf16[256,16,256]{2,1,0:T(8,128)(2,1)} async-done(((bf16[1,16,256]{2,1,0:T(8,128)(2,1)}), bf16[256,16,256]{2,1,0:T(8,128)(2,1)}) %all-gather.15.cloned.1.call-update) | async-done | bytes 2097168 | tf_op jit(solution)/shard_map/all_gather | solution.py:27
  6500.2 15.7 convert_bitcast_fusion.2
  6515.9 19.7 fusion.48
  6541.2 1280.9 %reduce-scatter.15.cloned.1.call-done = f32[1,16,256]{2,1,0:T(8,128)} async-done(((f32[256,16,256]{2,1,0:T(8,128)}), f32[1,16,256]{2,1,0:T(8,128)}) %reduce-scatter.15.cloned.1.call-update) | async-done | bytes 16400 | tf_op jit(solution)/shard_map/reduce_scatter | solution.py:31
  7823.4 81.0 psum.92
  7906.4 72.7 psum.93
  7980.5 100.7 %all-gather.17.cloned.1.call-done = bf16[256,16,256]{2,1,0:T(8,128)(2,1)} async-done(((bf16[1,16,256]{2,1,0:T(8,128)(2,1)}), bf16[256,16,256]{2,1,0:T(8,128)(2,1)}) %all-gather.17.cloned.1.call-update) | async-done | bytes 2097168 | tf_op jit(solution)/shard_map/all_gather | solution.py:27
  8106.2 19.8 fusion.51
  8131.6 1280.8 %reduce-scatter.17.cloned.1.call-done = f32[1,16,256]{2,1,0:T(8,128)} async-done(((f32[256,16,256]{2,1,0:T(8,128)}), f32[1,16,256]{2,1,0:T(8,128)}) %reduce-scatter.17.cloned.1.call-update) | async-done | bytes 16400 | tf_op jit(solution)/shard_map/reduce_scatter | solution.py:31
  9413.8 81.1 psum.94
  9496.8 72.7 psum.95
  (78 shorter events, 186.3 us)
Async XLA Ops:
  7.2 120.8 %copy-start = (bf16[6,256,256]{2,1,0:T(8,128)(2,1)S(1)}, bf16[6,256,256]{2,1,0:T(8,128)(2,1)}, u32[]{:S(2)}) copy-start(bf16[6,256,256]{2,1,0:T(8,128)(2,1)} %param.7) | copy-start | bytes 2359300
  7.2 120.8 %all-gather.7.cloned.1.call-start = ((), (), s32[]{:S(2)}) async-start(), calls=%async_computation.6 | async-start | bytes 2105344 | tf_op jit(solution)/shard_map/all_gather | solution.py:27
  7.2 130.2 %copy-start.1 = (bf16[6,16,16]{2,1,0:T(8,128)(2,1)S(1)}, bf16[6,16,16]{2,1,0:T(8,128)(2,1)}, u32[]{:S(2)}) copy-start(bf16[6,16,16]{2,1,0:T(8,128)(2,1)} %param.6) | copy-start | bytes 9220
  19.6 1442.5 %reduce-scatter.7.cloned.1.call-start = ((), (), s32[]{:S(2)}) async-start(), calls=%async_computation.7 | async-start | bytes 4210688 | tf_op jit(solution)/shard_map/reduce_scatter | solution.py:31
  137.4 15.6 copy-start.2
  178.3 1541.5 %all-gather.9.cloned.1.call-start = ((), (), s32[]{:S(2)}) async-start(), calls=%async_computation.8 | async-start | bytes 2105344 | tf_op jit(solution)/shard_map/all_gather | solution.py:27
  1619.8 1431.4 %reduce-scatter.9.cloned.1.call-start = ((), (), s32[]{:S(2)}) async-start(), calls=%async_computation.9 | async-start | bytes 4210688 | tf_op jit(solution)/shard_map/reduce_scatter | solution.py:31
  1770.4 1538.7 %all-gather.11.cloned.1.call-start = ((), (), s32[]{:S(2)}) async-start(), calls=%async_computation.10 | async-start | bytes 2105344 | tf_op jit(solution)/shard_map/all_gather | solution.py:27
  3208.4 1434.9 %reduce-scatter.11.cloned.1.call-start = ((), (), s32[]{:S(2)}) async-start(), calls=%async_computation.11 | async-start | bytes 4210688 | tf_op jit(solution)/shard_map/reduce_scatter | solution.py:31
  3359.6 1540.8 %all-gather.13.cloned.1.call-start = ((), (), s32[]{:S(2)}) async-start(), calls=%async_computation.12 | async-start | bytes 2105344 | tf_op jit(solution)/shard_map/all_gather | solution.py:27
  4800.4 1431.2 %reduce-scatter.13.cloned.1.call-start = ((), (), s32[]{:S(2)}) async-start(), calls=%async_computation.13 | async-start | bytes 4210688 | tf_op jit(solution)/shard_map/reduce_scatter | solution.py:31
  4950.7 1540.0 %all-gather.15.cloned.1.call-start = ((), (), s32[]{:S(2)}) async-start(), calls=%async_computation.14 | async-start | bytes 2105344 | tf_op jit(solution)/shard_map/all_gather | solution.py:27
  6390.0 1432.1 %reduce-scatter.15.cloned.1.call-start = ((), (), s32[]{:S(2)}) async-start(), calls=%async_computation.15 | async-start | bytes 4210688 | tf_op jit(solution)/shard_map/reduce_scatter | solution.py:31
  6541.2 1540.0 %all-gather.17.cloned.1.call-start = ((), (), s32[]{:S(2)}) async-start(), calls=%async_computation.16 | async-start | bytes 2105344 | tf_op jit(solution)/shard_map/all_gather | solution.py:27
  7980.4 1432.0 %reduce-scatter.17.cloned.1.call-start = ((), (), s32[]{:S(2)}) async-start(), calls=%async_computation.17 | async-start | bytes 4210688 | tf_op jit(solution)/shard_map/reduce_scatter | solution.py:31
Sparse Core Ops, SparseCore 0:
  19.7 108.1 all-gather.6
  178.5 1283.5 reduce-scatter.6
  1619.9 99.8 all-gather.8
  1770.5 1280.7 reduce-scatter.8
  3208.5 100.4 all-gather.10
  3359.7 1283.5 reduce-scatter.10
  4800.5 99.8 all-gather.12
  4950.8 1280.7 reduce-scatter.12
  6390.1 100.5 all-gather.14
  6541.3 1280.7 reduce-scatter.14
  7980.5 100.5 all-gather.16
  8131.6 1280.7 reduce-scatter.16
where the time goes:
time: 9590 us; the launch traced here: 9580 us
  waiting for transfers between devices  8300 us (87%)
  blocking collectives  919 us (10%)
  matrix products  269 us (3%)
    reduce_scatter x6, waiting for transfers between devices, local_run(): lax.psum_scatter(partial_sigma, 'terms', scatter_dimension=0, tiled=True)  7690 us
    all_gather x6, waiting for transfers between devices, local_run(): lax.all_gather(vector.astype(jnp.bfloat16), 'terms', axis=0, tiled=True)  610 us
    psum x6, blocking collectives, local_run(): alpha_val = lax.psum(jnp.sum(sigma_slab * vector), 'terms') / elem_count  479 us
    psum x6, blocking collectives, local_run(): lax.psum(jnp.sum(residual * residual), 'terms') / elem_count  439 us
  transfers between devices with their start and end apart: 12, of which 12 were waited for; matrix products, arithmetic and copies ran while one was open for 0% of the time, Pallas kernels for 0%

commit v1 on v0

v1 whole, which is shorter than its diff:
```python
import functools
import jax
import jax.numpy as jnp
from jax import lax
from jax.experimental import pallas as pl
from jax.experimental.pallas import tpu as pltpu
from jax.sharding import PartitionSpec as P

STEPS = 6
Z, Y, X, C = 8, 4, 4, 2
BOND, PAIR = 256, 16
OWN = 6
MEMB = X * C
GROUP = OWN * MEMB
SLAB = BOND // MEMB
COUNT = BOND * PAIR * BOND
F32, BF16 = jnp.float32, jnp.bfloat16
MESH = pl.DeviceIdType.MESH


def kernel(psi, left, wide, right, out, alphas, betas,
           lst, wall, rall, kron, u, vb, v, s, acc, yrecv, zsend, zrecv,
           loc_sem, l_send, l_recv, r_send, r_recv, rx_send, rs_send, rs_recv,
           ag_send, ag_recv, rl_send, rl_recv, d_send, d_recv):
    me = lax.axis_index("terms")
    c = lax.rem(me, C)
    x = lax.rem(me // C, X)
    y = lax.rem(me // (C * X), Y)
    z = me // (C * X * Y)
    mem = me % MEMB

    def dev(zz, yy, xx, cc):
        return (((zz * Y + yy) * X + xx) * C + cc,)

    def up(pos, step, size):
        return lax.rem(pos + step, size)

    def send(src, dst, ssem, rsem, to):
        copy = pltpu.make_async_remote_copy(src, dst, ssem, rsem, device_id=to, device_id_type=MESH)
        copy.start()
        return copy

    sib = dev(z, y, x, 1 - c)
    barrier = pltpu.get_barrier_semaphore()
    peers = [dev(up(z, d, Z), y, x, c) for d in range(1, Z)]
    peers += [dev(z, up(y, d, Y), x, c) for d in range(1, Y)]
    peers += [dev(z, y, up(x, d, X), cc) for d in range(1, X) for cc in range(C)]
    peers += [sib]
    for peer in peers:
        pl.semaphore_signal(barrier, inc=1, device_id=peer, device_id_type=MESH)

    own = pl.ds(OWN * mem, OWN)
    local = [pltpu.make_async_copy(psi, v.at[0], loc_sem.at[0]),
             pltpu.make_async_copy(left.at[:, pl.ds(pl.multiple_of(SLAB * mem, SLAB), SLAB)], lst.at[own], loc_sem.at[1]),
             pltpu.make_async_copy(right, rall.at[own], loc_sem.at[2]),
             pltpu.make_async_copy(wide, wall.at[own], loc_sem.at[3])]
    for copy in local:
        copy.start()
    pl.semaphore_wait(barrier, len(peers))

    half = OWN // 2

    def rblk(m, h):
        return rall.at[pl.ds(OWN * m + half * h, half)]

    xp, xm = up(x, 1, X), up(x, X - 1, X)
    early = []
    for d in range(MEMB - 1):
        to = lax.rem(mem + 1 + d, MEMB)
        early.append(send(left.at[:, pl.ds(pl.multiple_of(SLAB * to, SLAB), SLAB)], lst.at[own],
                          l_send.at[0, d], l_recv.at[0, d], dev(z, y, to // C, to % C)))
        early.append(send(wide, wall.at[own], l_send.at[1, d], l_recv.at[1, d], dev(z, y, to // C, to % C)))
    rp, rm, rd = [], [], []
    for h in (0, 1):
        src = right.at[pl.ds(half * h, half)]
        rp.append(send(src, rblk(mem, h), r_send.at[0, h], r_recv.at[0, h], dev(z, y, xp, c)))
        g = 1 - h
        src = right.at[pl.ds(half * g, half)]
        rm.append(send(src, rblk(mem, g), r_send.at[1, g], r_recv.at[1, g], dev(z, y, xm, c)))
    for h in (0, 1):
        rd.append(send(right.at[pl.ds(half * h, half)], rblk(mem, h), r_send.at[2, h], r_recv.at[2, h], sib))

    zero = jnp.zeros((64, BOND), F32)

    def clear(i, _):
        v[1, i // 4, pl.ds(pl.multiple_of((i % 4) * 64, 64), 64)] = zero
        return 0

    lax.fori_loop(0, 64, clear, 0)
    for copy in local:
        copy.wait()

    def vsl(i):
        return i // 4, pl.ds(pl.multiple_of((i % 4) * 64, 64), 64)

    def fold(t):
        return jnp.sum(t.reshape(8, 8, BOND), axis=0)

    def total(t):
        return jnp.sum(jnp.sum(t, axis=0, keepdims=True), axis=1, keepdims=True)

    def sq(i, t):
        q, r = vsl(i)
        blk = v[0, q, r]
        return t + fold(blk * blk)

    nrm = jnp.sqrt(total(lax.fori_loop(0, 64, sq, jnp.zeros((8, BOND), F32))) / COUNT)
    inv0 = 1.0 / nrm

    def scale0(i, _):
        q, r = vsl(i)
        blk = v[0, q, r] * inv0
        v[0, q, r] = blk
        vb[q, r] = blk.astype(BF16)
        return 0

    lax.fori_loop(0, 64, scale0, 0)

    def emit(row, slot):
        def one(q, _):
            out[row, pl.ds(q, 1)] = v[slot, q, pl.ds(me, 1)]
            return 0
        lax.fori_loop(0, PAIR, one, 0)

    emit(0, 0)
    for copy in early:
        copy.wait_recv()
    lane = lax.broadcasted_iota(jnp.int32, (16, 256), 1) % 16
    rowi = lax.broadcasted_iota(jnp.int32, (16, 256), 0)
    diag = lane == rowi

    def build(k, _):
        wk = wall[k].astype(F32)
        for q in range(PAIR):
            blk = jnp.where(diag, jnp.broadcast_to(wk[q:q + 1], (16, 256)), 0.0)
            kron[k, 16 * q:16 * q + 16] = blk.astype(BF16)
        return 0

    lax.fori_loop(0, GROUP, build, 0)

    mp, mm, m2 = C * xp + c, C * xm + c, C * up(x, 2, X) + c
    rp[0].wait_recv()
    fw = [send(rblk(mm, 0), rblk(mm, 0), rx_send.at[0], r_recv.at[3, 0], dev(z, y, xp, c)),
          send(rblk(mm, 0), rblk(mm, 0), rx_send.at[2], r_recv.at[4, 0], sib)]
    rm[0].wait_recv()
    fw += [send(rblk(mp, 1), rblk(mp, 1), rx_send.at[1], r_recv.at[3, 1], dev(z, y, xm, c)),
           send(rblk(mp, 1), rblk(mp, 1), rx_send.at[3], r_recv.at[4, 1], sib)]
    rp[1].wait_recv()
    fw += [send(rblk(mm, 1), rblk(mm, 1), rx_send.at[4], r_recv.at[5, 0], sib)]
    rm[1].wait_recv()
    fw += [send(rblk(mp, 0), rblk(mp, 0), rx_send.at[5], r_recv.at[5, 1], sib)]
    fw[0].wait_recv()
    fw += [send(rblk(m2, 0), rblk(m2, 0), rx_send.at[6], r_recv.at[6, 0], sib)]
    fw[2].wait_recv()
    fw += [send(rblk(m2, 1), rblk(m2, 1), rx_send.at[7], r_recv.at[6, 1], sib)]
    for copy in rd:
        copy.wait_recv()
    for i in (1, 3, 4, 5, 6, 7):
        fw[i].wait_recv()
    for copy in early + rp + rm + rd + fw:
        copy.wait_send()

    def matvec():
        def one(p, _):
            w = jnp.dot(lst[...].reshape(GROUP * SLAB, BOND), vb[p], preferred_element_type=F32)
            u[p] = w.astype(BF16).reshape(GROUP, SLAB, BOND)
            return 0
        lax.fori_loop(0, PAIR, one, 0)
        acc[...] = jnp.zeros_like(acc)
        UN = 4

        def terms(kk, _):
            res = None
            for i in range(UN):
                k = kk * UN + i
                zs = []
                for t in range(2):
                    blk = u[:, k, 16 * t:16 * t + 16].reshape(256, BOND)
                    zs.append(jnp.dot(kron[k], blk, preferred_element_type=F32).astype(BF16))
                o = jnp.dot(jnp.concatenate(zs, axis=0), rall[k], preferred_element_type=F32)
                res = o if res is None else res + o
            acc[...] += res.reshape(2, PAIR, 2, 8, BOND)
            return 0
        lax.fori_loop(0, GROUP // UN, terms, 0)

    def step(j, beta_prev):
        par = lax.rem(j, 2)
        matvec()
        ry = []
        for d in range(1, Y):
            yt = up(y, d, Y)
            ry.append(send(acc.at[yt // 2, :, yt % 2], yrecv.at[d - 1], rs_send.at[d - 1], rs_recv.at[d - 1], dev(z, yt, x, c)))
        for copy in ry:
            copy.wait_recv()
        ysum = acc[y // 2, :, y % 2] + yrecv[0] + yrecv[1] + yrecv[2]
        zsend[...] = ysum.reshape(Z, 2, 8, BOND)
        rz = []
        for d in range(1, Z):
            zt = up(z, d, Z)
            rz.append(send(zsend.at[zt], zrecv.at[d - 1], rs_send.at[2 + d], rs_recv.at[2 + d], dev(zt, y, x, c)))
        for copy in rz:
            copy.wait_recv()
        zsum = zsend[z]
        for d in range(Z - 1):
            zsum = zsum + zrecv[d]
        s[par, pl.ds(2 * z, 2), x, c, y] = zsum

        sent = list(ry) + list(rz)
        ch = s.at[par, pl.ds(2 * z, 2), x, c, y]
        gz = [send(ch, ch, ag_send.at[par, d - 1], ag_recv.at[par, d - 1], dev(up(z, d, Z), y, x, c)) for d in range(1, Z)]
        for copy in gz:
            copy.wait_recv()
        sent += gz
        lo, hi = pl.ds(0, 128), pl.ds(128, 128)
        q0, q1, qa = pl.ds(0, 8), pl.ds(8, 8), pl.ds(0, 16)
        yp, ym, y2 = up(y, 1, Y), up(y, Y - 1, Y), up(y, 2, Y)
        x2 = up(x, 2, X)
        tyP, tyM = dev(z, yp, x, c), dev(z, ym, x, c)
        txP, txM = dev(z, y, xp, c), dev(z, y, xm, c)

        def a2(yy, q):
            return s.at[par, q, x, c, yy, :, lo]

        def b2(xx, q):
            return s.at[par, q, xx, c, y, :, hi]

        def a3(xx, q):
            return s.at[par, q, xx, c, :, :, lo]

        def b3(yy, q):
            return s.at[par, q, :, c, yy, :, hi]

        def go(ref, i, to):
            copy = send(ref, ref, rl_send.at[par, i], rl_recv.at[par, i], to)
            sent.append(copy)
            return copy

        def ring2(fa, fb, base):
            (f, own_, p_, m_, tP, tM), (g, gown, gp_, gm_, sP, sM) = fa, fb
            k = [go(f(own_, qa), base, tP), go(f(own_, qa), base + 1, tM),
                 go(g(gown, qa), base + 2, sP), go(g(gown, qa), base + 3, sM)]
            k[0].wait_recv()
            k.append(go(f(m_, q0), base + 4, tP))
            k[1].wait_recv()
            k.append(go(f(p_, q1), base + 5, tM))
            k[2].wait_recv()
            k.append(go(g(gm_, q0), base + 6, sP))
            k[3].wait_recv()
            k.append(go(g(gp_, q1), base + 7, sM))
            return k[4:]

        for copy in ring2((a2, y, yp, ym, tyP, tyM), (b2, x, xp, xm, txP, txM), 0):
            copy.wait_recv()
        dd = []

        def cross(ref, i):
            copy = send(ref, ref, d_send.at[par, i], d_recv.at[par, i], sib)
            sent.append(copy)
            dd.append(copy)

        k3 = ring2((a3, x, xp, xm, txP, txM), (b3, y, yp, ym, tyP, tyM), 8)
        cross(a3(x, qa), 0)
        cross(b3(y, qa), 1)
        cross(a3(xm, qa), 2)
        cross(a3(xp, qa), 3)
        cross(b3(ym, qa), 4)
        cross(b3(yp, qa), 5)
        k3[0].wait_recv()
        k3[1].wait_recv()
        cross(a3(x2, qa), 6)
        k3[2].wait_recv()
        k3[3].wait_recv()
        cross(b3(y2, qa), 7)
        for copy in dd:
            copy.wait_recv()
        for copy in sent:
            copy.wait_send()

        cur, prev = lax.rem(j, 2), lax.rem(j + 1, 2)

        def sload(i):
            return s[par, i // 4, i % 4].reshape(64, BOND)

        def dot_sv(i, t):
            q, r = vsl(i)
            return t + fold(sload(i) * v[cur, q, r])

        alpha = total(lax.fori_loop(0, 64, dot_sv, jnp.zeros((8, BOND), F32))) / COUNT

        def resid(i, t):
            q, r = vsl(i)
            w = sload(i) - alpha * v[cur, q, r] - beta_prev * v[prev, q, r]
            v[prev, q, r] = w
            return t + fold(w * w)

        beta = jnp.sqrt(total(lax.fori_loop(0, 64, resid, jnp.zeros((8, BOND), F32))) / COUNT)
        inv = 1.0 / beta

        def scale(i, _):
            q, r = vsl(i)
            w = v[prev, q, r] * inv
            v[prev, q, r] = w
            vb[q, r] = w.astype(BF16)
            return 0

        lax.fori_loop(0, 64, scale, 0)
        emit(j + 1, prev)
        alphas[j] = alpha[0, 0]
        betas[j] = beta[0, 0]
        return beta

    lax.fori_loop(0, STEPS, step, jnp.zeros((1, 1), F32))


def solution(mesh):
    def local_run(psi_init, left_env, op_pair, right_env):
        psi_t = jnp.transpose(psi_init.reshape(BOND, PAIR, BOND), (1, 0, 2))
        wide = jnp.repeat(op_pair, 16, axis=2)
        dma = pltpu.SemaphoreType.DMA
        any_ = pl.BlockSpec(memory_space=pl.ANY)
        out, al, be = pl.pallas_call(
            kernel,
            out_shape=(jax.ShapeDtypeStruct((STEPS + 1, PAIR, BOND), F32),
                       jax.ShapeDtypeStruct((STEPS,), F32),
                       jax.ShapeDtypeStruct((STEPS,), F32)),
            in_specs=[any_] * 4,
            out_specs=(pl.BlockSpec(memory_space=pltpu.VMEM),
                       pl.BlockSpec(memory_space=pltpu.SMEM),
                       pl.BlockSpec(memory_space=pltpu.SMEM)),
            scratch_shapes=[
                pltpu.VMEM((GROUP, SLAB, BOND), BF16),
                pltpu.VMEM((GROUP, PAIR, 256), BF16),
                pltpu.VMEM((GROUP, BOND, BOND), BF16),
                pltpu.VMEM((GROUP, 256, 256), BF16),
                pltpu.VMEM((PAIR, GROUP, SLAB, BOND), BF16),
                pltpu.VMEM((PAIR, BOND, BOND), BF16),
                pltpu.VMEM((2, PAIR, BOND, BOND), F32),
                pltpu.VMEM((2, PAIR, X, C, Y, 8, BOND), F32),
                pltpu.VMEM((2, PAIR, 2, 8, BOND), F32),
                pltpu.VMEM((Y - 1, PAIR, 8, BOND), F32),
                pltpu.VMEM((Z, 2, 8, BOND), F32),
                pltpu.VMEM((Z - 1, 2, 8, BOND), F32),
                dma((4,)), dma((2, 7)), dma((2, 7)),
                dma((3, 2)), dma((7, 2)), dma((8,)),
                dma((10,)), dma((10,)),
                dma((2, 7)), dma((2, 7)),
                dma((2, 16)), dma((2, 16)),
                dma((2, 8)), dma((2, 8)),
            ],
            compiler_params=pltpu.CompilerParams(
                collective_id=0, has_side_effects=True, vmem_limit_bytes=66 * 1000 * 1000),
        )(psi_t, left_env, wide, right_env)
        return out.reshape(STEPS + 1, 1, 4, 4, BOND), al, be

    return jax.shard_map(local_run, mesh=mesh, in_specs=(P(), P("terms"), P("terms"), P("terms")),
                         out_specs=(P(None, "terms"), P(), P()), check_vma=False)
```

time: 9590 us -> 444 us (0.05)
  waiting for transfers between devices: 8300 us -> 0 us
  blocking collectives: 919 us -> 0 us
  Pallas kernels: 0 us -> 430 us
  matrix products: 269 us -> 0 us
    reduce_scatter x6 -> x0, waiting for transfers between devices: 7690 us -> none  [local_run(): lax.psum_scatter(partial_sigma, 'terms', scatter_dimension=0, tiled=True)]
    psum x12 -> x0, blocking collectives: 919 us -> none  [the longest x6 479 us: local_run(): alpha_val = lax.psum(jnp.sum(sigma_slab * vector), 'terms') / elem_count]
    all_gather x6 -> x0, waiting for transfers between devices: 610 us -> none  [local_run(): lax.all_gather(vector.astype(jnp.bfloat16), 'terms', axis=0, tiled=True)]
    pallas_call x0 -> x1, Pallas kernels: none -> 430 us  [local_run(): pl.pallas_call(kernel, out_shape=(jax.ShapeDtypeStruct((STEPS + 1, PAIR,...]
    dot_general x18 -> x0, matrix products: 269 us -> none  [the longest x6 119 us: local_run(): jnp.einsum('kax,kxqb->aqb', left_env, z_part, preferred_element_type=jnp....]
  transfers between devices with their start and end apart: 12 -> 0, of which waited for: 12 -> 0; matrix products, arithmetic and copies ran while one was open for 0% -> 0% of each run, Pallas kernels for 0% -> 0%
where the time goes in v1:
time: 444 us; the launch traced here: 443 us
  Pallas kernels  430 us (97%)
  local copies, waits for them, and re-layouts  12.4 us (3%)
    pallas_call x1, Pallas kernels, local_run(): pl.pallas_call(kernel, out_shape=(jax.ShapeDtypeStruct((STEPS + 1, PAIR,...  430 us

profile of v1, /device:TPU:1, one launch (start us, length us, event | category | flops | bytes accessed | tf_op | source)
XLA Modules:
  0.0 443.4 jit_solution(12134556334748662876)
XLA Ops:
  0.6 1.0 broadcast_in_dim.3
  1.6 1.0 reshape.16.wide
  2.6 6.6 %copy.7 = f32[256,4,4,256]{3,0,2,1:T(8,128)} copy(f32[256,4,4,256]{3,2,1,0:T(4,128)} %param.4) | data formatting | bytes 8388608 | tf_op args[0]
  9.2 430.4 %shard_map.67 = (f32[7,16,256]{2,1,0:T(8,128)}, f32[6]{0:T(128)}, f32[6]{0:T(128)}) custom-call(f32[16,256,256]{2,1,0:T(8,128)} %bitcast.6, bf16[6,256,256]{2,1,0:T(8,128)(2,1)} %left.1, bf16[6,16,256]{2,1,0:T(8,128)(2,1)} %reshape.16.wide, bf16[6,256,256]{2,1,0:T(8,128)(2,1)} %right.1), custom_call_target="tpu_custom_call" | custom-call | tf_op jit(solution)/shard_map/pallas_call | solution.py:321
  439.6 1.6 reshape.17
  441.2 1.1 copy.11
  442.3 1.1 copy.12

commit v2 on v0

v2 whole, which is shorter than its diff:
```python
import jax
import jax.numpy as jnp
from jax import lax
from jax.experimental import pallas as pl
from jax.experimental.pallas import tpu as pltpu
from jax.sharding import PartitionSpec as P

STEPS = 6
Z, Y, X, C = 8, 4, 4, 2
BOND, PAIR = 256, 16
OWN = 6
MEMB = X * C
GROUP = OWN * MEMB
SLAB = BOND // MEMB
PART = 3
PT = OWN // PART
COUNT = BOND * PAIR * BOND
UNROLL = 24
QY = PAIR // Y
DIRECT2 = ("2",)
F32, BF16 = jnp.float32, jnp.bfloat16
MESH = pl.DeviceIdType.MESH


class Span:
    def __init__(self):
        self.open = None

    def __call__(self, name):
        if self.open is not None:
            self.open.__exit__(None, None, None)
        self.open = None
        if name:
            self.open = jax.named_scope(name)
            self.open.__enter__()


def kernel(psi, left, ops, right, out, scalars,
           lst, wall, wide, rall, kron, u, vb, v, s, acc, yrecv, zsend, zrecv, ssend, srecv, ay, az, am, rown, rsib, rrecv,
           loc_sem, l_send, l_recv, r_send, r_recv, y_send, y_recv, z_send, z_recv,
           gz_send, gz_recv, gr_send, gr_recv, c_send, c_recv, a_send, a_recv, b_send, b_recv, row_send, row_recv):
    me = lax.axis_index("terms")
    sp = Span()
    c = lax.rem(me, C)
    x = lax.rem(me // C, X)
    y = lax.rem(me // (C * X), Y)
    z = me // (C * X * Y)
    mem = lax.rem(me, MEMB)

    def dev(zz, yy, xx, cc):
        return (((zz * Y + yy) * X + xx) * C + cc,)

    def up(pos, step, size):
        return lax.rem(pos + step, size)

    def send(src, dst, ssem, rsem, to):
        copy = pltpu.make_async_remote_copy(src, dst, ssem, rsem, device_id=to, device_id_type=MESH)
        copy.start()
        return copy

    xp, xm, x2 = up(x, 1, X), up(x, X - 1, X), up(x, 2, X)
    yp, ym, y2 = up(y, 1, Y), up(y, Y - 1, Y), up(y, 2, Y)
    sib = dev(z, y, x, 1 - c)
    txp, txm = dev(z, y, xp, c), dev(z, y, xm, c)
    typ, tym = dev(z, yp, x, c), dev(z, ym, x, c)

    sp("entry")
    barrier = pltpu.get_barrier_semaphore()
    peers = [dev(up(z, d, Z), y, x, c) for d in range(1, Z)]
    peers += [dev(z, up(y, d, Y), x, c) for d in range(1, Y)]
    peers += [dev(z, y, up(x, d, X), cc) for d in range(1, X) for cc in range(C)]
    peers += [sib]
    for peer in peers:
        pl.semaphore_signal(barrier, inc=1, device_id=peer, device_id_type=MESH)
    own = pl.ds(OWN * mem, OWN)
    local = [pltpu.make_async_copy(psi.at[:, c, :, p // 4, p % 4, :], v.at[0, p], loc_sem.at[4 + p]) for p in range(PAIR)]
    local = local[::-1] + [
             pltpu.make_async_copy(left.at[:, pl.ds(pl.multiple_of(SLAB * mem, SLAB), SLAB)], lst.at[own], loc_sem.at[1]),
             pltpu.make_async_copy(right, rall.at[own], loc_sem.at[2]),
             pltpu.make_async_copy(ops, wall.at[own], loc_sem.at[3])]
    for copy in local:
        copy.start()
    pl.semaphore_wait(barrier, len(peers))

    early = []
    for d in range(MEMB - 1):
        to = lax.rem(mem + 1 + d, MEMB)
        early.append(send(left.at[:, pl.ds(pl.multiple_of(SLAB * to, SLAB), SLAB)], lst.at[own],
                          l_send.at[0, d], l_recv.at[0, d], dev(z, y, to // C, lax.rem(to, C))))
        early.append(send(ops, wall.at[own], l_send.at[1, d], l_recv.at[1, d],
                          dev(z, y, to // C, lax.rem(to, C))))

    def rpart(m, h):
        return rall.at[pl.ds(OWN * m + PT * h, PT)]

    pend = []
    H = BOND // 2

    def quads(ref, k0):
        return ref.at[pl.ds(k0, PT), pl.ds(0, H)], ref.at[pl.ds(k0, PT), pl.ds(H, H), pl.ds(H, H)]

    def rsend(src, dst, i, kind, to):
        copy = send(src, dst, r_send.at[i, kind], r_recv.at[i, kind], to)
        pend.append(copy)
        return copy

    def qsend(src, k0, m, h, i, to, kinds=(0, 1)):
        a, b = quads(src, k0), quads(rall, OWN * m + PT * h)
        return [rsend(a[kind], b[kind], i, kind, to) for kind in kinds]

    def mirror(m, h):
        for i in range(PT):
            k = OWN * m + PT * h + i
            rall[k, H:, :H] = rall[k, :H, H:].T

    def rpart(m, h):
        return rall.at[pl.ds(OWN * m + PT * h, PT)]

    from_xm, from_xp, from_sib = {}, {}, {}
    for h in range(PART):
        g = PART - 1 - h
        from_xm[h] = qsend(right, PT * h, mem, h, h, txp)
        from_xp[g] = qsend(right, PT * g, mem, g, PART + g, txm)
    for h in range(PART):
        from_sib[h] = rsend(right.at[pl.ds(PT * h, PT)], rpart(mem, h), 2 * PART + h, 0, sib)

    def chunk(i):
        return i // 2, pl.ds((i % 2) * 2, 2)

    NCH = 2 * PAIR

    def vload(slot, i):
        q, xx = chunk(i)
        return v[slot, q, xx].reshape(64, BOND)

    def vstore(slot, i, val):
        q, xx = chunk(i)
        v[slot, q, xx] = val.reshape(2, SLAB, BOND)

    def sload(par, i):
        q, xx = chunk(i)
        return s[par, q, xx].reshape(64, BOND)

    def fold(t):
        return jnp.sum(t.reshape(8, 8, BOND), axis=0)

    def both(part, i):
        tile = part[:, :128] + part[:, 128:]
        ssend[i] = tile
        copy = send(ssend.at[i], srecv.at[i], c_send.at[i], c_recv.at[i], sib)
        copy.wait()
        t = tile + srecv[i]
        return jnp.sum(jnp.sum(t, axis=0, keepdims=True), axis=1, keepdims=True)

    inhalf = me // (BOND // X)

    other = me + 1 - 2 * c
    QG = PAIR // 4

    def vbcopy(g):
        ref = vb.at[pl.ds(QG * g, QG), :, c]
        return pltpu.make_async_remote_copy(ref, ref, b_send.at[g], b_recv.at[g], device_id=sib, device_id_type=MESH)

    def finish(slot, inv, row):
        copies = []
        for g in range(4):
            def one(i, _):
                w = vload(slot, i) * inv
                vstore(slot, i, w)
                q, xx = chunk(i)
                vb[q, xx, c] = w.astype(BF16).reshape(2, SLAB, BOND)
                return 0
            lax.fori_loop(NCH // 4 * g, NCH // 4 * (g + 1), one, 0, unroll=2)
            copies.append(vbcopy(g))
            copies[-1].start()

        def pick(q, _):
            rown[row, pl.ds(q, 1)] = v[slot, q, inhalf, pl.ds(lax.rem(me, SLAB), 1)]
            rsib[row, pl.ds(q, 1)] = v[slot, q, inhalf, pl.ds(lax.rem(other, SLAB), 1)]
            return 0

        lax.fori_loop(0, PAIR, pick, 0, unroll=4)
        copies.append(send(rsib.at[row], rrecv.at[row], row_send.at[0], row_recv.at[0], sib))
        return copies

    def first(copies):
        rows = lst[...].reshape(GROUP * SLAB, BOND)
        for g in range(4):
            copies[g].wait_recv()
            for p in range(QG * g, QG * g + QG):
                w = jnp.dot(rows, vb[p].reshape(BOND, BOND), preferred_element_type=F32)
                u[p] = w.astype(BF16).reshape(GROUP, SLAB, BOND)
        settle(copies, 4)

    def settle(copies, n):
        for copy in copies[n:]:
            copy.wait_recv()
        for copy in copies:
            copy.wait_send()

    sp("init")
    for copy in local:
        copy.wait()

    def sq(i, t):
        blk = vload(0, i)
        return t + fold(blk * blk)

    def clear(i, _):
        vstore(1, i, jnp.zeros((64, BOND), F32))
        return 0

    lax.fori_loop(0, NCH, clear, 0)
    part = lax.fori_loop(0, NCH, sq, jnp.zeros((8, BOND), F32), unroll=2)
    nrm = jnp.sqrt(both(part, 0) / COUNT)
    begun = finish(0, 1.0 / nrm, 0)

    sp("waitL")
    for copy in early:
        copy.wait_recv()
    sp("build")
    lane = lax.broadcasted_iota(jnp.int32, (16, 256), 1) % 16
    rowi = lax.broadcasted_iota(jnp.int32, (16, 256), 0)
    diag = lane == rowi

    spread = lax.broadcasted_iota(jnp.int32, (PAIR, 256), 0) == lax.broadcasted_iota(jnp.int32, (PAIR, 256), 1) // 16
    rows = jnp.dot(wall[...].reshape(GROUP * PAIR, PAIR), spread.astype(F32).astype(BF16), preferred_element_type=F32)
    wide[...] = rows.reshape(GROUP, PAIR, 256)

    def build(k, _):
        wk = wide[k]
        for q in range(PAIR):
            blk = jnp.where(diag, jnp.broadcast_to(wk[q:q + 1], (16, 256)), 0.0)
            kron[k, 16 * q:16 * q + 16] = blk.astype(BF16)
        return 0

    lax.fori_loop(0, GROUP, build, 0)

    def rest(ks, ts):
        res = None
        for k in ks:
            zs = []
            for t in ts:
                blk = u[:, k, 16 * t:16 * t + 16].reshape(256, BOND)
                zs.append(jnp.dot(kron[k], blk, preferred_element_type=F32).astype(BF16))
            zk = zs[0] if len(zs) == 1 else jnp.concatenate(zs, axis=0)
            o = jnp.dot(zk, rall[k], preferred_element_type=F32)
            res = o if res is None else res + o
        for i, t in enumerate(ts):
            acc[t] += res[256 * i:256 * i + 256].reshape(Y, QY, 16, BOND)

    def ycopy(t, d):
        yt = up(y, d, Y)
        return pltpu.make_async_remote_copy(acc.at[t, yt], yrecv.at[t, d - 1], y_send.at[t, d - 1], y_recv.at[t, d - 1],
                                            device_id=dev(z, yt, x, c), device_id_type=MESH)

    def ystart(t):
        for d in range(1, Y):
            ycopy(t, d).start()

    def adot(t, slot):
        part = jnp.zeros((8, BOND), F32)
        for q in range(PAIR):
            prod = acc[t, q // QY, q % QY] * v[slot, q, x, 16 * t:16 * t + 16]
            part = part + prod[:8] + prod[8:]
        return part

    def acopy(stage, par, d):
        if stage == 0:
            ref, to = ay.at[y], dev(z, up(y, d, Y), x, c)
        elif stage == 1:
            ref, to = az.at[z], dev(up(z, d, Z), y, x, c)
        else:
            other_ = lax.rem(mem + d, MEMB)
            ref, to = am.at[par, mem], dev(z, y, other_ // C, lax.rem(other_, C))
        i = (0, Y - 1, Y + Z - 2)[stage] + d - 1
        return pltpu.make_async_remote_copy(ref, ref, a_send.at[par, i], a_recv.at[par, i], device_id=to, device_id_type=MESH)

    ASIZE = (Y, Z, MEMB)

    def astart(stage, par, tile):
        if stage == 0:
            ay[y] = tile
        elif stage == 1:
            az[z] = tile
        else:
            am[par, mem] = tile
        for d in range(1, ASIZE[stage]):
            acopy(stage, par, d).start()

    def adone(stage, par):
        for d in range(1, ASIZE[stage]):
            acopy(stage, par, d).wait_recv()
        tile = None
        for i in range(ASIZE[stage]):
            one_ = ay[i] if stage == 0 else az[i] if stage == 1 else am[par, i]
            tile = one_ if tile is None else tile + one_
        return tile

    def abegin(par, slot):
        part = adot(0, slot) + adot(1, slot)
        astart(0, par, part[:, :128] + part[:, 128:])

    def block(t):
        acc[t] = jnp.zeros((Y, QY, 16, BOND), F32)

        def some(kk, _):
            rest([kk * UNROLL + i for i in range(UNROLL)], [t])
            return 0
        lax.fori_loop(0, GROUP // UNROLL, some, 0)
        ystart(t)

    def tail(j, beta_prev, last):
        st = Span()
        par = lax.rem(j, 2)
        sent = []
        hz = lax.rem(z, 2)
        qz = QY * y + z // 2

        def ydone(t):
            for d in range(1, Y):
                ycopy(t, d).wait_recv()
            ysum = acc[t, y] + yrecv[t, 0] + yrecv[t, 1] + yrecv[t, 2]
            zsend[t] = ysum.reshape(Z, 8, BOND)
            zc = []
            for d in range(1, Z):
                zt = up(z, d, Z)
                zc.append(send(zsend.at[t, zt], zrecv.at[t, d - 1], z_send.at[t, d - 1], z_recv.at[t, d - 1], dev(zt, y, x, c)))
            sent.extend(zc)
            return zc

        def zdone(t, zc):
            for copy in zc:
                copy.wait_recv()
            zsum = zsend[t, z]
            for d in range(Z - 1):
                zsum = zsum + zrecv[t, d]
            s[par, qz, x, t, hz] = zsum
            ch = s.at[par, qz, x, t, hz]
            gz = [send(ch, ch, gz_send.at[par, t, d - 1], gz_recv.at[par, t, d - 1], dev(up(z, d, Z), y, x, c))
                  for d in range(1, Z)]
            sent.extend(gz)
            return gz

        slot = [0]

        def piece(part, i, k, q):
            t, h = part
            xx, yy = (k, i) if h == 0 else (i, k)
            return s.at[par, pl.ds(QY * yy + q[0], q[1]), xx, t, :, :, pl.ds(128 * h, 128)]

        qa, q0, q1 = (0, QY), (0, QY // 2), (QY // 2, QY // 2)

        def go(ref, to):
            i = slot[0]
            slot[0] += 1
            copy = send(ref, ref, gr_send.at[par, i], gr_recv.at[par, i], to)
            sent.append(copy)
            return copy

        ax = [((y, yp, ym, y2, typ, tym), (x, xp, xm, x2, txp, txm)),
              ((x, xp, xm, x2, txp, txm), (y, yp, ym, y2, typ, tym))]
        far = [dev(z, y2, x, c), dev(z, y, x2, c)]
        one, two, rel2 = {}, {}, {}

        def second(part, i, tag):
            (_, (w, _, _, _, tp, tm)) = ax[part[1]]
            two[part, tag] = [go(piece(part, i, w, qa), tp), go(piece(part, i, w, qa), tm), i]
            if tag in DIRECT2:
                two[part, tag].append(go(piece(part, i, w, qa), far[1 - part[1]]))

        def relay2(part, tag):
            (_, (w, wp, wm, _, tp, tm)) = ax[part[1]]
            cp, cm, i, *direct = two[part, tag]
            cp.wait_recv()
            if direct:
                cm.wait_recv()
                rel2[part, tag] = direct
                return
            a = go(piece(part, i, wm, q0), tp)
            cm.wait_recv()
            b = go(piece(part, i, wp, q1), tm)
            rel2[part, tag] = [a, b]

        def open_(t, gz):
            for copy in gz:
                copy.wait_recv()
            for h in (0, 1):
                ((w, _, _, _, tp, tm), (k, *_)) = ax[h]
                one[t, h] = [go(piece((t, h), w, k, qa), to) for to in (tp, tm, far[h])]
            for h in (0, 1):
                second((t, h), ax[h][0][0], "own")

        def near(t):
            for h in (0, 1):
                ((w, wp, wm, _, tp, tm), (k, *_)) = ax[h]
                one[t, h][0].wait_recv()
                second((t, h), wm, "m")
                one[t, h][1].wait_recv()
                second((t, h), wp, "p")

        def distant(t):
            for h in (0, 1):
                one[t, h][2].wait_recv()
                second((t, h), ax[h][0][3], "2")

        def relays(t, tag):
            for h in (0, 1):
                relay2((t, h), tag)

        st("rs0")
        z0 = ydone(0)
        st("rs1")
        z1 = ydone(1)
        astart(1, par, adone(0, par))
        st("z0")
        g0 = zdone(0, z0)
        st("z1")
        plane = adone(1, par)
        g1 = zdone(1, z1)
        astart(2, par, plane)
        st("g0")
        open_(0, g0)
        st("g1")
        open_(1, g1)
        st("n0")
        near(0)
        st("n1")
        near(1)
        st("o0")
        relays(0, "own")
        distant(0)
        st("o1")
        relays(1, "own")
        distant(1)
        st("ag3")
        for tag in ("m", "p", "2"):
            for t in (0, 1):
                relays(t, tag)
        for t in (0, 1):
            for tag in ("own", "m", "p", "2"):
                for h in (0, 1):
                    for copy in rel2[(t, h), tag]:
                        copy.wait_recv()
        st("sendw")
        for copy in sent:
            copy.wait_send()
        for t in (0, 1):
            for d in range(1, Y):
                ycopy(t, d).wait_send()

        st("v1")
        cur, prev = lax.rem(j, 2), lax.rem(j + 1, 2)
        tile = adone(2, par)
        alpha = jnp.sum(jnp.sum(tile, axis=0, keepdims=True), axis=1, keepdims=True) / COUNT
        for stage in range(3):
            for d in range(1, ASIZE[stage]):
                acopy(stage, par, d).wait_send()
        st("v2")

        def resid(i, t):
            w = sload(par, i) - alpha * vload(cur, i) - beta_prev * vload(prev, i)
            vstore(prev, i, w)
            return t + fold(w * w)

        part = lax.fori_loop(0, NCH, resid, jnp.zeros((8, BOND), F32), unroll=2)
        st("xb")
        beta = jnp.sqrt(both(part, 1) / COUNT)
        st("v3")
        copies = finish(prev, 1.0 / beta, j + 1)
        scalars[0, j] = alpha[0, 0]
        scalars[1, j] = beta[0, 0]
        if last:
            settle(copies, 0)
        else:
            st("stage1")
            first(copies)
            st("block0")
            block(0)
            st("block1")
            block(1)
            abegin(lax.rem(j + 1, 2), prev)
        st("")
        return beta

    sp("first")
    first(begun)
    acc[...] = jnp.zeros_like(acc)
    msib = C * x + 1 - c
    mm, mp, m2 = C * xm + c, C * xp + c, C * x2 + c
    sm, sq_, s2 = C * xm + 1 - c, C * xp + 1 - c, C * x2 + 1 - c
    base = 3 * PART

    def terms(m, h):
        return [OWN * m + PT * h + i for i in range(PT)]

    def arrive(copies, m, h, i, on=()):
        for copy in copies:
            copy.wait_recv()
        far_ = []
        for slot_, to, kinds in on:
            far_ += qsend(rall, OWN * m + PT * h, m, h, slot_, to, kinds)
        mirror(m, h)
        return far_, rsend(rpart(m, h), rpart(m, h), i, 0, sib)

    sp("R0")
    far0, a0 = arrive(from_xm[0], mm, 0, base + 3, [(base + 0, txp, (0, 1))])
    far2, b2 = arrive(from_xp[2], mp, 2, base + 8, [(base + 2, txm, (0, 1))])
    for h in range(PART):
        from_sib[h].wait_recv()
    rest([k for h in range(PART) for m in (mem, msib) for k in terms(m, h)], (0, 1))
    sp("R1")
    far1b, a1 = arrive(from_xm[1], mm, 1, base + 4, [(base + 1, txp, (1,))])
    far1a, b1 = arrive(from_xp[1], mp, 1, base + 7, [(base + 1, txm, (0,))])
    a0.wait_recv()
    b2.wait_recv()
    rest(terms(mm, 0) + terms(sm, 0) + terms(mp, 2) + terms(sq_, 2), (0, 1))
    sp("R2")
    _, a2 = arrive(from_xm[2], mm, 2, base + 5)
    _, b0 = arrive(from_xp[0], mp, 0, base + 6)
    a1.wait_recv()
    b1.wait_recv()
    rest(terms(mm, 1) + terms(sm, 1) + terms(mp, 1) + terms(sq_, 1), (0, 1))
    sp("R3")
    _, f0 = arrive(far0, m2, 0, base + 9)
    _, f2 = arrive(far2, m2, 2, base + 11)
    a2.wait_recv()
    b0.wait_recv()
    rest(terms(mm, 2) + terms(sm, 2) + terms(mp, 0) + terms(sq_, 0), (0, 1))
    sp("R4")
    _, f1 = arrive(far1a + far1b, m2, 1, base + 10)
    f0.wait_recv()
    f2.wait_recv()
    rest(terms(m2, 0) + terms(s2, 0) + terms(m2, 2) + terms(s2, 2), (0, 1))
    sp("R5")
    f1.wait_recv()
    rest(terms(m2, 1) + terms(s2, 1), (0, 1))
    for copy in early + pend:
        copy.wait_send()
    sp("")

    ystart(0)
    ystart(1)
    abegin(0, 0)

    def step(j, beta_prev):
        return tail(j, beta_prev, False)

    tail(STEPS - 1, lax.fori_loop(0, STEPS - 1, step, jnp.zeros((1, 1), F32)), True)
    mine = lax.rem(me // SLAB, C) == c
    out[...] = jnp.where(mine, rown[...], rrecv[...])


def solution(mesh):
    def local_run(psi_init, left_env, op_pair, right_env):
        dma = pltpu.SemaphoreType.DMA
        any_ = pl.BlockSpec(memory_space=pl.ANY)
        rows = pltpu.VMEM((STEPS + 1, PAIR, BOND), F32)
        out, scalars = pl.pallas_call(
            kernel,
            out_shape=(jax.ShapeDtypeStruct((STEPS + 1, PAIR, BOND), F32),
                       jax.ShapeDtypeStruct((2, STEPS), F32)),
            in_specs=[any_] * 4,
            out_specs=(pl.BlockSpec(memory_space=pltpu.VMEM),
                       pl.BlockSpec(memory_space=pltpu.SMEM)),
            scratch_shapes=[
                pltpu.VMEM((GROUP, SLAB, BOND), BF16),
                pltpu.VMEM((GROUP, PAIR, PAIR), BF16),
                pltpu.VMEM((GROUP, PAIR, 256), F32),
                pltpu.VMEM((GROUP, BOND, BOND), BF16),
                pltpu.VMEM((GROUP, 256, 256), BF16),
                pltpu.VMEM((PAIR, GROUP, SLAB, BOND), BF16),
                pltpu.VMEM((PAIR, X, C, SLAB, BOND), BF16),
                pltpu.VMEM((2, PAIR, X, SLAB, BOND), F32),
                pltpu.VMEM((2, PAIR, X, 2, 2, 8, BOND), F32),
                pltpu.VMEM((2, Y, QY, 16, BOND), F32),
                pltpu.VMEM((2, Y - 1, QY, 16, BOND), F32),
                pltpu.VMEM((2, Z, 8, BOND), F32),
                pltpu.VMEM((2, Z - 1, 8, BOND), F32),
                pltpu.VMEM((2, 8, 128), F32),
                pltpu.VMEM((2, 8, 128), F32),
                pltpu.VMEM((Y, 8, 128), F32),
                pltpu.VMEM((Z, 8, 128), F32),
                pltpu.VMEM((2, MEMB, 8, 128), F32),
                rows, rows, rows,
                dma((20,)), dma((2, 7)), dma((2, 7)),
                dma((21, 2)), dma((21, 2)),
                dma((2, 3)), dma((2, 3)), dma((2, 7)), dma((2, 7)),
                dma((2, 2, 7)), dma((2, 2, 7)),
                dma((2, 80)), dma((2, 80)),
                dma((2,)), dma((2,)),
                dma((2, 17)), dma((2, 17)),
                dma((4,)), dma((4,)),
                dma((1,)), dma((1,)),
            ],
            compiler_params=pltpu.CompilerParams(
                collective_id=0, has_side_effects=True, vmem_limit_bytes=66 * 1000 * 1000),
        )(psi_init.reshape(X, C, SLAB, 4, 4, BOND), left_env, op_pair, right_env)
        return out.reshape(STEPS + 1, 1, 4, 4, BOND), scalars[0], scalars[1]

    return jax.shard_map(local_run, mesh=mesh, in_specs=(P(), P("terms"), P("terms"), P("terms")),
                         out_specs=(P(None, "terms"), P(), P()), check_vma=False)
```

time: 9590 us -> 311 us (0.03)
  waiting for transfers between devices: 8300 us -> 0 us
  blocking collectives: 919 us -> 0 us
  Pallas kernels: 0 us -> 307 us
  matrix products: 269 us -> 0 us
    reduce_scatter x6 -> x0, waiting for transfers between devices: 7690 us -> none  [local_run(): lax.psum_scatter(partial_sigma, 'terms', scatter_dimension=0, tiled=True)]
    psum x12 -> x0, blocking collectives: 919 us -> none  [the longest x6 479 us: local_run(): alpha_val = lax.psum(jnp.sum(sigma_slab * vector), 'terms') / elem_count]
    all_gather x6 -> x0, waiting for transfers between devices: 610 us -> none  [local_run(): lax.all_gather(vector.astype(jnp.bfloat16), 'terms', axis=0, tiled=True)]
    pallas_call x0 -> x1, Pallas kernels: none -> 307 us  [local_run(): pl.pallas_call(kernel, out_shape=(jax.ShapeDtypeStruct((STEPS + 1, PAIR,...]
    dot_general x18 -> x0, matrix products: 269 us -> none  [the longest x6 119 us: local_run(): jnp.einsum('kax,kxqb->aqb', left_env, z_part, preferred_element_type=jnp....]
  transfers between devices with their start and end apart: 12 -> 0, of which waited for: 12 -> 0; matrix products, arithmetic and copies ran while one was open for 0% -> 0% of each run, Pallas kernels for 0% -> 0%
where the time goes in v2:
time: 311 us; the launch traced here: 310 us
  Pallas kernels  307 us (99%)
    pallas_call x1, Pallas kernels, local_run(): pl.pallas_call(kernel, out_shape=(jax.ShapeDtypeStruct((STEPS + 1, PAIR,...  307 us

profile of v2, /device:TPU:1, one launch (start us, length us, event | category | flops | bytes accessed | tf_op | source)
XLA Modules:
  0.0 310.4 jit_solution(626116475224696629)
XLA Ops:
  0.6 306.9 %shard_map.67 = (f32[7,16,256]{2,1,0:T(8,128)}, f32[2,6]{1,0:T(2,128)}) custom-call(f32[4,2,32,4,4,256]{5,4,3,2,1,0:T(4,128)} %bitcast.6, bf16[6,256,256]{2,1,0:T(8,128)(2,1)} %left.1, bf16[6,16,16]{2,1,0:T(8,128)(2,1)} %ops.1, bf16[6,256,256]{2,1,0:T(8,128)(2,1)} %right.1), custom_call_target="tpu_custom_call" | custom-call | tf_op jit(solution)/shard_map/pallas_call | solution.py:559
  307.5 1.6 reshape.13
  309.1 1.3 slice_bitcast_fusion

commit v3 on v2

--- a/solution.py
+++ b/solution.py
@@ -17,7 +17,7 @@
 COUNT = BOND * PAIR * BOND
 UNROLL = 24
 QY = PAIR // Y
-DIRECT2 = ("2",)
+DIRECT2 = ((), ("2",))
 F32, BF16 = jnp.float32, jnp.bfloat16
 MESH = pl.DeviceIdType.MESH
 
@@ -36,8 +36,8 @@
 
 
 def kernel(psi, left, ops, right, out, scalars,
-           lst, wall, wide, rall, kron, u, vb, v, s, acc, yrecv, zsend, zrecv, ssend, srecv, ay, az, am, rown, rsib, rrecv,
-           loc_sem, l_send, l_recv, r_send, r_recv, y_send, y_recv, z_send, z_recv,
+           lst, wall, wide, rall, kron, u, vb, v, s, acc, accin, yrecv, zsend, zrecv, ssend, srecv, ay, az, am, rown, rsib, rrecv,
+           loc_sem, l_send, l_recv, r_send, r_recv, x_send, x_recv, y_send, y_recv, z_send, z_recv,
            gz_send, gz_recv, gr_send, gr_recv, c_send, c_recv, a_send, a_recv, b_send, b_recv, row_send, row_recv):
     me = lax.axis_index("terms")
     sp = Span()
@@ -73,7 +73,7 @@
     for peer in peers:
         pl.semaphore_signal(barrier, inc=1, device_id=peer, device_id_type=MESH)
     own = pl.ds(OWN * mem, OWN)
-    local = [pltpu.make_async_copy(psi.at[:, c, :, p // 4, p % 4, :], v.at[0, p], loc_sem.at[4 + p]) for p in range(PAIR)]
+    local = [pltpu.make_async_copy(psi.at[:, :, c, :, p // 4, p % 4, :], v.at[0, p], loc_sem.at[4 + p]) for p in range(PAIR)]
     local = local[::-1] + [
              pltpu.make_async_copy(left.at[:, pl.ds(pl.multiple_of(SLAB * mem, SLAB), SLAB)], lst.at[own], loc_sem.at[1]),
              pltpu.make_async_copy(right, rall.at[own], loc_sem.at[2]),
@@ -135,7 +135,7 @@
 
     def vstore(slot, i, val):
         q, xx = chunk(i)
-        v[slot, q, xx] = val.reshape(2, SLAB, BOND)
+        v[slot, q, xx] = val.reshape(2, C, 16, BOND)
 
     def sload(par, i):
         q, xx = chunk(i)
@@ -158,7 +158,7 @@
     QG = PAIR // 4
 
     def vbcopy(g):
-        ref = vb.at[pl.ds(QG * g, QG), :, c]
+        ref = vb.at[pl.ds(QG * g, QG), :, :, c]
         return pltpu.make_async_remote_copy(ref, ref, b_send.at[g], b_recv.at[g], device_id=sib, device_id_type=MESH)
 
     def finish(slot, inv, row):
@@ -168,15 +168,15 @@
                 w = vload(slot, i) * inv
                 vstore(slot, i, w)
                 q, xx = chunk(i)
-                vb[q, xx, c] = w.astype(BF16).reshape(2, SLAB, BOND)
+                vb[q, xx, :, c] = w.astype(BF16).reshape(2, C, 16, BOND)
                 return 0
             lax.fori_loop(NCH // 4 * g, NCH // 4 * (g + 1), one, 0, unroll=2)
             copies.append(vbcopy(g))
             copies[-1].start()
 
         def pick(q, _):
-            rown[row, pl.ds(q, 1)] = v[slot, q, inhalf, pl.ds(lax.rem(me, SLAB), 1)]
-            rsib[row, pl.ds(q, 1)] = v[slot, q, inhalf, pl.ds(lax.rem(other, SLAB), 1)]
+            rown[row, pl.ds(q, 1)] = v[slot, q, inhalf, lax.rem(me // SLAB, C), pl.ds(lax.rem(me, 16), 1)]
+            rsib[row, pl.ds(q, 1)] = v[slot, q, inhalf, lax.rem(me // SLAB, C), pl.ds(lax.rem(other, 16), 1)]
             return 0
 
         lax.fori_loop(0, PAIR, pick, 0, unroll=4)
@@ -249,9 +249,18 @@
         for i, t in enumerate(ts):
             acc[t] += res[256 * i:256 * i + 256].reshape(Y, QY, 16, BOND)
 
+    slab = (c, 1 - c)
+
+    def handover():
+        return pltpu.make_async_remote_copy(acc.at[1 - c], accin, x_send.at[0], x_recv.at[0],
+                                            device_id=sib, device_id_type=MESH)
+
+    def mine_(t, *i):
+        return acc[(c, *i)] if t == 0 else accin[i]
+
     def ycopy(t, d):
         yt = up(y, d, Y)
-        return pltpu.make_async_remote_copy(acc.at[t, yt], yrecv.at[t, d - 1], y_send.at[t, d - 1], y_recv.at[t, d - 1],
+        return pltpu.make_async_remote_copy(acc.at[c, yt] if t == 0 else accin.at[yt], yrecv.at[t, d - 1], y_send.at[t, d - 1], y_recv.at[t, d - 1],
                                             device_id=dev(z, yt, x, c), device_id_type=MESH)
 
     def ystart(t):
@@ -261,15 +270,15 @@
     def adot(t, slot):
         part = jnp.zeros((8, BOND), F32)
         for q in range(PAIR):
-            prod = acc[t, q // QY, q % QY] * v[slot, q, x, 16 * t:16 * t + 16]
+            prod = mine_(t, q // QY, q % QY) * v[slot, q, x, slab[t]]
             part = part + prod[:8] + prod[8:]
         return part
 
     def acopy(stage, par, d):
         if stage == 0:
-            ref, to = ay.at[y], dev(z, up(y, d, Y), x, c)
+            ref, to = ay.at[par, y], dev(z, up(y, d, Y), x, c)
         elif stage == 1:
-            ref, to = az.at[z], dev(up(z, d, Z), y, x, c)
+            ref, to = az.at[par, z], dev(up(z, d, Z), y, x, c)
         else:
             other_ = lax.rem(mem + d, MEMB)
             ref, to = am.at[par, mem], dev(z, y, other_ // C, lax.rem(other_, C))
@@ -280,9 +289,9 @@
 
     def astart(stage, par, tile):
         if stage == 0:
-            ay[y] = tile
+            ay[par, y] = tile
         elif stage == 1:
-            az[z] = tile
+            az[par, z] = tile
         else:
             am[par, mem] = tile
         for d in range(1, ASIZE[stage]):
@@ -293,7 +302,7 @@
             acopy(stage, par, d).wait_recv()
         tile = None
         for i in range(ASIZE[stage]):
-            one_ = ay[i] if stage == 0 else az[i] if stage == 1 else am[par, i]
+            one_ = ay[par, i] if stage == 0 else az[par, i] if stage == 1 else am[par, i]
             tile = one_ if tile is None else tile + one_
         return tile
 
@@ -301,14 +310,27 @@
         part = adot(0, slot) + adot(1, slot)
         astart(0, par, part[:, :128] + part[:, 128:])
 
-    def block(t):
-        acc[t] = jnp.zeros((Y, QY, 16, BOND), F32)
-
-        def some(kk, _):
-            rest([kk * UNROLL + i for i in range(UNROLL)], [t])
-            return 0
-        lax.fori_loop(0, GROUP // UNROLL, some, 0)
-        ystart(t)
+    def on(core, *acts):
+        @pl.when(c == core)
+        def _():
+            for act in acts:
+                act()
+
+    def take():
+        handover().wait_recv()
+        ystart(1)
+
+    def blocks():
+        acc[...] = jnp.zeros_like(acc)
+
+        rest(list(range(GROUP)), [0])
+        on(1, lambda: handover().start())
+        on(0, lambda: ystart(0))
+        rest(list(range(UNROLL)), [1])
+        on(0, take)
+        rest(list(range(UNROLL, GROUP)), [1])
+        on(1, lambda: ystart(0))
+        on(0, lambda: handover().start())
 
     def tail(j, beta_prev, last):
         st = Span()
@@ -320,7 +342,7 @@
         def ydone(t):
             for d in range(1, Y):
                 ycopy(t, d).wait_recv()
-            ysum = acc[t, y] + yrecv[t, 0] + yrecv[t, 1] + yrecv[t, 2]
+            ysum = mine_(t, y) + yrecv[t, 0] + yrecv[t, 1] + yrecv[t, 2]
             zsend[t] = ysum.reshape(Z, 8, BOND)
             zc = []
             for d in range(1, Z):
@@ -335,8 +357,8 @@
             zsum = zsend[t, z]
             for d in range(Z - 1):
                 zsum = zsum + zrecv[t, d]
-            s[par, qz, x, t, hz] = zsum
-            ch = s.at[par, qz, x, t, hz]
+            s[par, qz, x, slab[t], hz] = zsum
+            ch = s.at[par, qz, x, slab[t], hz]
             gz = [send(ch, ch, gz_send.at[par, t, d - 1], gz_recv.at[par, t, d - 1], dev(up(z, d, Z), y, x, c))
                   for d in range(1, Z)]
             sent.extend(gz)
@@ -347,7 +369,7 @@
         def piece(part, i, k, q):
             t, h = part
             xx, yy = (k, i) if h == 0 else (i, k)
-            return s.at[par, pl.ds(QY * yy + q[0], q[1]), xx, t, :, :, pl.ds(128 * h, 128)]
+            return s.at[par, pl.ds(QY * yy + q[0], q[1]), xx, slab[t], :, :, pl.ds(128 * h, 128)]
 
         qa, q0, q1 = (0, QY), (0, QY // 2), (QY // 2, QY // 2)
 
@@ -366,7 +388,7 @@
         def second(part, i, tag):
             (_, (w, _, _, _, tp, tm)) = ax[part[1]]
             two[part, tag] = [go(piece(part, i, w, qa), tp), go(piece(part, i, w, qa), tm), i]
-            if tag in DIRECT2:
+            if tag in DIRECT2[part[0]]:
                 two[part, tag].append(go(piece(part, i, w, qa), far[1 - part[1]]))
 
         def relay2(part, tag):
@@ -408,21 +430,23 @@
             for h in (0, 1):
                 relay2((t, h), tag)
 
+        st("take")
+        on(1, take)
+        abegin(par, par)
         st("rs0")
         z0 = ydone(0)
         st("rs1")
         z1 = ydone(1)
-        astart(1, par, adone(0, par))
         st("z0")
         g0 = zdone(0, z0)
+        astart(1, par, adone(0, par))
         st("z1")
-        plane = adone(1, par)
         g1 = zdone(1, z1)
-        astart(2, par, plane)
         st("g0")
         open_(0, g0)
         st("g1")
         open_(1, g1)
+        astart(2, par, adone(1, par))
         st("n0")
         near(0)
         st("n1")
@@ -448,6 +472,7 @@
         for t in (0, 1):
             for d in range(1, Y):
                 ycopy(t, d).wait_send()
+        handover().wait_send()
 
         st("v1")
         cur, prev = lax.rem(j, 2), lax.rem(j + 1, 2)
@@ -475,11 +500,8 @@
         else:
             st("stage1")
             first(copies)
-            st("block0")
-            block(0)
-            st("block1")
-            block(1)
-            abegin(lax.rem(j + 1, 2), prev)
+            st("blocks")
+            blocks()
         st("")
         return beta
 
@@ -539,15 +561,15 @@
         copy.wait_send()
     sp("")
 
+    handover().start()
     ystart(0)
-    ystart(1)
-    abegin(0, 0)
+    on(0, take)
 
     def step(j, beta_prev):
         return tail(j, beta_prev, False)
 
     tail(STEPS - 1, lax.fori_loop(0, STEPS - 1, step, jnp.zeros((1, 1), F32)), True)
-    mine = lax.rem(me // SLAB, C) == c
+    mine = lax.rem(me // 16, 2) == c
     out[...] = jnp.where(mine, rown[...], rrecv[...])
 
 
@@ -570,21 +592,23 @@
                 pltpu.VMEM((GROUP, BOND, BOND), BF16),
                 pltpu.VMEM((GROUP, 256, 256), BF16),
                 pltpu.VMEM((PAIR, GROUP, SLAB, BOND), BF16),
-                pltpu.VMEM((PAIR, X, C, SLAB, BOND), BF16),
-                pltpu.VMEM((2, PAIR, X, SLAB, BOND), F32),
-                pltpu.VMEM((2, PAIR, X, 2, 2, 8, BOND), F32),
+                pltpu.VMEM((PAIR, X, C, 2, 16, BOND), BF16),
+                pltpu.VMEM((2, PAIR, X, C, 16, BOND), F32),
+                pltpu.VMEM((2, PAIR, X, C, 2, 8, BOND), F32),
                 pltpu.VMEM((2, Y, QY, 16, BOND), F32),
+                pltpu.VMEM((Y, QY, 16, BOND), F32),
                 pltpu.VMEM((2, Y - 1, QY, 16, BOND), F32),
                 pltpu.VMEM((2, Z, 8, BOND), F32),
                 pltpu.VMEM((2, Z - 1, 8, BOND), F32),
                 pltpu.VMEM((2, 8, 128), F32),
                 pltpu.VMEM((2, 8, 128), F32),
-                pltpu.VMEM((Y, 8, 128), F32),
-                pltpu.VMEM((Z, 8, 128), F32),
+                pltpu.VMEM((2, Y, 8, 128), F32),
+                pltpu.VMEM((2, Z, 8, 128), F32),
                 pltpu.VMEM((2, MEMB, 8, 128), F32),
                 rows, rows, rows,
                 dma((20,)), dma((2, 7)), dma((2, 7)),
                 dma((21, 2)), dma((21, 2)),
+                dma((1,)), dma((1,)),
                 dma((2, 3)), dma((2, 3)), dma((2, 7)), dma((2, 7)),
                 dma((2, 2, 7)), dma((2, 2, 7)),
                 dma((2, 80)), dma((2, 80)),
@@ -595,7 +619,7 @@
             ],
             compiler_params=pltpu.CompilerParams(
                 collective_id=0, has_side_effects=True, vmem_limit_bytes=66 * 1000 * 1000),
-        )(psi_init.reshape(X, C, SLAB, 4, 4, BOND), left_env, op_pair, right_env)
+        )(psi_init.reshape(X, C, 2, 16, 4, 4, BOND), left_env, op_pair, right_env)
         return out.reshape(STEPS + 1, 1, 4, 4, BOND), scalars[0], scalars[1]
 
     return jax.shard_map(local_run, mesh=mesh, in_specs=(P(), P("terms"), P("terms"), P("terms")),

time: 311 us -> 297 us (0.955)
  Pallas kernels: 307 us -> 294 us
    pallas_call x1, Pallas kernels: 307 us -> 294 us  [local_run(): pl.pallas_call(kernel, out_shape=(jax.ShapeDtypeStruct((STEPS + 1, PAIR,...]
where the time goes in v3:
time: 297 us
  Pallas kernels  294 us (99%)
    pallas_call x1, Pallas kernels, local_run(): pl.pallas_call(kernel, out_shape=(jax.ShapeDtypeStruct((STEPS + 1, PAIR,...  294 us

profile of v3, /device:TPU:1, one launch (start us, length us, event | category | flops | bytes accessed | tf_op | source)
XLA Modules:
  0.0 297.3 jit_solution(13147953623064225921)
XLA Ops:
  0.6 293.9 %shard_map.67 = (f32[7,16,256]{2,1,0:T(8,128)}, f32[2,6]{1,0:T(2,128)}) custom-call(f32[4,2,2,16,4,4,256]{6,5,4,3,2,1,0:T(4,128)} %bitcast.6, bf16[6,256,256]{2,1,0:T(8,128)(2,1)} %left.1, bf16[6,16,16]{2,1,0:T(8,128)(2,1)} %ops.1, bf16[6,256,256]{2,1,0:T(8,128)(2,1)} %right.1), custom_call_target="tpu_custom_call" | custom-call | tf_op jit(solution)/shard_map/pallas_call | solution.py:581
  294.5 1.6 reshape.13
  296.1 1.3 slice_bitcast_fusion

commit v4 on v3

--- a/solution.py
+++ b/solution.py
@@ -16,6 +16,7 @@
 PT = OWN // PART
 COUNT = BOND * PAIR * BOND
 UNROLL = 24
+PLANE = Y * X * C
 QY = PAIR // Y
 DIRECT2 = ((), ("2",))
 F32, BF16 = jnp.float32, jnp.bfloat16
@@ -36,9 +37,9 @@
 
 
 def kernel(psi, left, ops, right, out, scalars,
-           lst, wall, wide, rall, kron, u, vb, v, s, acc, accin, yrecv, zsend, zrecv, ssend, srecv, ay, az, am, rown, rsib, rrecv,
+           lst, wall, wide, rall, kron, u, vb, v, s, acc, accin, yrecv, zsend, zrecv, ssend, srecv, pm, zm, rown, rsib, rrecv,
            loc_sem, l_send, l_recv, r_send, r_recv, x_send, x_recv, y_send, y_recv, z_send, z_recv,
-           gz_send, gz_recv, gr_send, gr_recv, c_send, c_recv, a_send, a_recv, b_send, b_recv, row_send, row_recv):
+           gz_send, gz_recv, gr_send, gr_recv, c_send, c_recv, p_send, p_recv, a_send, a_recv, b_send, b_recv, row_send, row_recv):
     me = lax.axis_index("terms")
     sp = Span()
     c = lax.rem(me, C)
@@ -67,9 +68,8 @@
     sp("entry")
     barrier = pltpu.get_barrier_semaphore()
     peers = [dev(up(z, d, Z), y, x, c) for d in range(1, Z)]
-    peers += [dev(z, up(y, d, Y), x, c) for d in range(1, Y)]
-    peers += [dev(z, y, up(x, d, X), cc) for d in range(1, X) for cc in range(C)]
-    peers += [sib]
+    place = lax.rem(me, PLANE)
+    peers += [(PLANE * z + lax.rem(place + d, PLANE),) for d in range(1, PLANE)]
     for peer in peers:
         pl.semaphore_signal(barrier, inc=1, device_id=peer, device_id_type=MESH)
     own = pl.ds(OWN * mem, OWN)
@@ -144,12 +144,11 @@
     def fold(t):
         return jnp.sum(t.reshape(8, 8, BOND), axis=0)
 
-    def both(part, i):
+    def both(part):
         tile = part[:, :128] + part[:, 128:]
-        ssend[i] = tile
-        copy = send(ssend.at[i], srecv.at[i], c_send.at[i], c_recv.at[i], sib)
-        copy.wait()
-        t = tile + srecv[i]
+        ssend[...] = tile
+        send(ssend, srecv, c_send.at[0], c_recv.at[0], sib).wait()
+        t = tile + srecv[...]
         return jnp.sum(jnp.sum(t, axis=0, keepdims=True), axis=1, keepdims=True)
 
     inhalf = me // (BOND // X)
@@ -161,11 +160,11 @@
         ref = vb.at[pl.ds(QG * g, QG), :, :, c]
         return pltpu.make_async_remote_copy(ref, ref, b_send.at[g], b_recv.at[g], device_id=sib, device_id_type=MESH)
 
-    def finish(slot, inv, row):
+    def finish(slot, value, row):
         copies = []
         for g in range(4):
             def one(i, _):
-                w = vload(slot, i) * inv
+                w = value(i)
                 vstore(slot, i, w)
                 q, xx = chunk(i)
                 vb[q, xx, :, c] = w.astype(BF16).reshape(2, C, 16, BOND)
@@ -212,8 +211,9 @@
 
     lax.fori_loop(0, NCH, clear, 0)
     part = lax.fori_loop(0, NCH, sq, jnp.zeros((8, BOND), F32), unroll=2)
-    nrm = jnp.sqrt(both(part, 0) / COUNT)
-    begun = finish(0, 1.0 / nrm, 0)
+    nrm = jnp.sqrt(both(part) / COUNT)
+    inv0 = 1.0 / nrm
+    begun = finish(0, lambda i: vload(0, i) * inv0, 0)
 
     sp("waitL")
     for copy in early:
@@ -274,41 +274,43 @@
             part = part + prod[:8] + prod[8:]
         return part
 
-    def acopy(stage, par, d):
-        if stage == 0:
-            ref, to = ay.at[par, y], dev(z, up(y, d, Y), x, c)
-        elif stage == 1:
-            ref, to = az.at[par, z], dev(up(z, d, Z), y, x, c)
+    def acopy(which, par, d):
+        if d < PLANE:
+            ref, to = pm.at[which, place], (PLANE * z + lax.rem(place + d, PLANE),)
+            sems = p_send.at[which, d - 1], p_recv.at[which, d - 1]
         else:
-            other_ = lax.rem(mem + d, MEMB)
-            ref, to = am.at[par, mem], dev(z, y, other_ // C, lax.rem(other_, C))
-        i = (0, Y - 1, Y + Z - 2)[stage] + d - 1
-        return pltpu.make_async_remote_copy(ref, ref, a_send.at[par, i], a_recv.at[par, i], device_id=to, device_id_type=MESH)
-
-    ASIZE = (Y, Z, MEMB)
-
-    def astart(stage, par, tile):
-        if stage == 0:
-            ay[par, y] = tile
-        elif stage == 1:
-            az[par, z] = tile
-        else:
-            am[par, mem] = tile
-        for d in range(1, ASIZE[stage]):
-            acopy(stage, par, d).start()
-
-    def adone(stage, par):
-        for d in range(1, ASIZE[stage]):
-            acopy(stage, par, d).wait_recv()
-        tile = None
-        for i in range(ASIZE[stage]):
-            one_ = ay[par, i] if stage == 0 else az[par, i] if stage == 1 else am[par, i]
-            tile = one_ if tile is None else tile + one_
-        return tile
+            d = d - PLANE + 1
+            ref, to = zm.at[par, which, z], dev(up(z, d, Z), y, x, c)
+            sems = a_send.at[par, which, d - 1], a_recv.at[par, which, d - 1]
+        return pltpu.make_async_remote_copy(ref, ref, *sems, device_id=to, device_id_type=MESH)
+
+    IN_PLANE, IN_Z = range(1, PLANE), range(PLANE, PLANE + Z - 1)
+
+    def plane_start(which, par, part):
+        pm[which, place] = jnp.sum(part[:, :128] + part[:, 128:], axis=0, keepdims=True)
+        for d in IN_PLANE:
+            acopy(which, par, d).start()
+
+    def plane_done(which, par):
+        for d in IN_PLANE:
+            acopy(which, par, d).wait_recv()
+        sums = [pm[which, i] for i in range(PLANE)]
+        while len(sums) > 1:
+            sums = [a + b for a, b in zip(sums[::2], sums[1::2])]
+        zm[par, which, z] = sums[0]
+        for d in IN_Z:
+            acopy(which, par, d).start()
+
+    def scalar(which, par):
+        for d in IN_Z:
+            acopy(which, par, d).wait_recv()
+        sums = [zm[par, which, i] for i in range(Z)]
+        while len(sums) > 1:
+            sums = [a + b for a, b in zip(sums[::2], sums[1::2])]
+        return jnp.sum(sums[0], axis=1, keepdims=True) / COUNT
 
     def abegin(par, slot):
-        part = adot(0, slot) + adot(1, slot)
-        astart(0, par, part[:, :128] + part[:, 128:])
+        plane_start(0, par, adot(0, slot) + adot(1, slot))
 
     def on(core, *acts):
         @pl.when(c == core)
@@ -439,14 +441,22 @@
         z1 = ydone(1)
         st("z0")
         g0 = zdone(0, z0)
-        astart(1, par, adone(0, par))
+        plane_done(0, par)
         st("z1")
         g1 = zdone(1, z1)
         st("g0")
         open_(0, g0)
         st("g1")
         open_(1, g1)
-        astart(2, par, adone(1, par))
+        cur, prev = lax.rem(j, 2), lax.rem(j + 1, 2)
+        alpha = scalar(0, par)
+        part = jnp.zeros((8, BOND), F32)
+        rows8 = pl.ds(pl.multiple_of(8 * hz, 8), 8)
+        for t in (0, 1):
+            w = (s[par, qz, x, slab[t], hz] - alpha * v[cur, qz, x, slab[t], rows8]
+                 - beta_prev * v[prev, qz, x, slab[t], rows8])
+            part = part + w * w
+        plane_start(1, par, part)
         st("n0")
         near(0)
         st("n1")
@@ -457,6 +467,7 @@
         st("o1")
         relays(1, "own")
         distant(1)
+        plane_done(1, par)
         st("ag3")
         for tag in ("m", "p", "2"):
             for t in (0, 1):
@@ -466,35 +477,26 @@
                 for h in (0, 1):
                     for copy in rel2[(t, h), tag]:
                         copy.wait_recv()
-        st("sendw")
-        for copy in sent:
-            copy.wait_send()
+        st("beta")
+        beta = jnp.sqrt(scalar(1, par))
+        inv = 1.0 / beta
         for t in (0, 1):
             for d in range(1, Y):
                 ycopy(t, d).wait_send()
         handover().wait_send()
-
-        st("v1")
-        cur, prev = lax.rem(j, 2), lax.rem(j + 1, 2)
-        tile = adone(2, par)
-        alpha = jnp.sum(jnp.sum(tile, axis=0, keepdims=True), axis=1, keepdims=True) / COUNT
-        for stage in range(3):
-            for d in range(1, ASIZE[stage]):
-                acopy(stage, par, d).wait_send()
-        st("v2")
-
-        def resid(i, t):
-            w = sload(par, i) - alpha * vload(cur, i) - beta_prev * vload(prev, i)
-            vstore(prev, i, w)
-            return t + fold(w * w)
-
-        part = lax.fori_loop(0, NCH, resid, jnp.zeros((8, BOND), F32), unroll=2)
-        st("xb")
-        beta = jnp.sqrt(both(part, 1) / COUNT)
         st("v3")
-        copies = finish(prev, 1.0 / beta, j + 1)
+
+        def value(i):
+            return (sload(par, i) - alpha * vload(cur, i) - beta_prev * vload(prev, i)) * inv
+
+        copies = finish(prev, value, j + 1)
         scalars[0, j] = alpha[0, 0]
         scalars[1, j] = beta[0, 0]
+        for copy in sent:
+            copy.wait_send()
+        for which in (0, 1):
+            for d in (*IN_PLANE, *IN_Z):
+                acopy(which, par, d).wait_send()
         if last:
             settle(copies, 0)
         else:
@@ -600,11 +602,10 @@
                 pltpu.VMEM((2, Y - 1, QY, 16, BOND), F32),
                 pltpu.VMEM((2, Z, 8, BOND), F32),
                 pltpu.VMEM((2, Z - 1, 8, BOND), F32),
-                pltpu.VMEM((2, 8, 128), F32),
-                pltpu.VMEM((2, 8, 128), F32),
-                pltpu.VMEM((2, Y, 8, 128), F32),
-                pltpu.VMEM((2, Z, 8, 128), F32),
-                pltpu.VMEM((2, MEMB, 8, 128), F32),
+                pltpu.VMEM((8, 128), F32),
+                pltpu.VMEM((8, 128), F32),
+                pltpu.VMEM((2, PLANE, 1, 128), F32),
+                pltpu.VMEM((2, 2, Z, 1, 128), F32),
                 rows, rows, rows,
                 dma((20,)), dma((2, 7)), dma((2, 7)),
                 dma((21, 2)), dma((21, 2)),
@@ -612,8 +613,8 @@
                 dma((2, 3)), dma((2, 3)), dma((2, 7)), dma((2, 7)),
                 dma((2, 2, 7)), dma((2, 2, 7)),
                 dma((2, 80)), dma((2, 80)),
-                dma((2,)), dma((2,)),
-                dma((2, 17)), dma((2, 17)),
+                dma((1,)), dma((1,)),
+                dma((2, PLANE - 1)), dma((2, PLANE - 1)), dma((2, 2, Z - 1)), dma((2, 2, Z - 1)),
                 dma((4,)), dma((4,)),
                 dma((1,)), dma((1,)),
             ],

time: 297 us -> 291 us (0.980)
  Pallas kernels: 294 us -> 288 us
    pallas_call x1, Pallas kernels: 294 us -> 288 us  [local_run(): pl.pallas_call(kernel, out_shape=(jax.ShapeDtypeStruct((STEPS + 1, PAIR,...]
where the time goes in v4:
time: 291 us
  Pallas kernels  288 us (99%)
    pallas_call x1, Pallas kernels, local_run(): pl.pallas_call(kernel, out_shape=(jax.ShapeDtypeStruct((STEPS + 1, PAIR,...  288 us

profile of v4, /device:TPU:1, one launch (start us, length us, event | category | flops | bytes accessed | tf_op | source)
XLA Modules:
  0.0 291.0 jit_solution(4343084972201469406)
XLA Ops:
  0.6 287.5 %shard_map.67 = (f32[7,16,256]{2,1,0:T(8,128)}, f32[2,6]{1,0:T(2,128)}) custom-call(f32[4,2,2,16,4,4,256]{6,5,4,3,2,1,0:T(4,128)} %bitcast.6, bf16[6,256,256]{2,1,0:T(8,128)(2,1)} %left.1, bf16[6,16,16]{2,1,0:T(8,128)(2,1)} %ops.1, bf16[6,256,256]{2,1,0:T(8,128)(2,1)} %right.1), custom_call_target="tpu_custom_call" | custom-call | tf_op jit(solution)/shard_map/pallas_call | solution.py:583
  288.2 1.6 reshape.13
  289.8 1.3 slice_bitcast_fusion
